TPU v7x, 512 devices: a whole 4x8x8 slice. The times are simulated.
512 devices in a mesh: seq: 128 (over y, z, core), head: 4 (over x).
Axes of the slice: x: 4, y: 8, z: 8, core: 2. Of those that a mesh axis runs over, the one named last changes fastest.
Arguments:
- hidden_states: bfloat16 [8, 8192, 3584], P(None, 'seq', 'head'), may hold values from -6 to 6
- boundary: int32 [8, 64], replicated, may hold values from 0 to 8191, as said below
- valid: int32 [8, 64], replicated, may hold values from 0 to 1, as said below
- pairs: int32 [8, 2], replicated, may hold values from 0 to 7, as said below
- w_first: bfloat16 [3584, 4096], P('seq', 'head'), may hold values from -0.09375 to 0.09375
- b_first: float32 [4096], P('head'), may hold values from -3 to 3
- w_second: float32 [4096], P('head'), may hold values from -0.09375 to 0.09375
Outputs:
- step_reward: float32 [8, 64], replicated
- trace_score: float32 [8], replicated
- margin: float32 [8], replicated
Inputs may be any that keep to these rules, and one draw needn't show every extreme that they name: Within a trace the 64 boundary positions are distinct and increasing. In each trace the ones come first; every trace has 16 to 64 valid steps. `pairs`: the two traces of a pair differ.
All inputs are finite; a program needn't handle non-finite values.
Results may differ from a plain program's by a relative error of at most 0.0003.
Values may be sent and summed in bfloat16 or wider, within the bound.
No kernel may reach another device: no remote copies, remote signals or barrier semaphores. Data moves between devices by JAX's collectives and lax.ppermute only.
A program may use at most 64 MiB of HBM per device.

v0:
```python
import jax
import jax.numpy as jnp
from jax import lax
from jax.sharding import Mesh
from jax.sharding import PartitionSpec as P

SEQ = ("seq_0", "seq_1", "seq_2")
SEQ_HEAD = ("seq_0", "seq_1", "seq_2", "head")


def laid_out(pieces, dim):
    pieces = jnp.moveaxis(pieces, 0, dim)
    shape = pieces.shape
    return pieces.reshape(*shape[:dim], shape[dim] * shape[dim + 1], *shape[dim + 2 :])


def sent_to_all(shard, axis):
    copies = jnp.broadcast_to(shard, (lax.axis_size(axis), *shard.shape))
    return lax.all_to_all(copies, axis, split_axis=0, concat_axis=0, tiled=True)


def gather_directly(shard, axis, dim):
    return laid_out(sent_to_all(shard, axis), dim)


def over_axes(shard, axes):
    for axis in axes:
        shard = lax.psum(shard, axis)
    return shard


def score_rows(rows, w_first, b_first, w_second):
    pre = jnp.dot(
        rows, lax.all_gather(w_first, SEQ, axis=0, tiled=True), preferred_element_type=jnp.float32
    )
    return jnp.sum(jnp.maximum(pre + b_first, 0.0) * w_second, axis=-1)


def per_device(hidden_states, boundary, valid, pairs, w_first, b_first, w_second):
    traces, tok_dev, quarter = hidden_states.shape
    offset = lax.axis_index(SEQ) * tok_dev
    positions = offset + jnp.arange(tok_dev, dtype=jnp.int32)
    hits = boundary[:, :, None] == positions[None, None, :]
    whole = gather_directly(hidden_states, "head", 2)
    token_logit = score_rows(
        whole.reshape(traces * tok_dev, whole.shape[2]), w_first, b_first, w_second
    )
    token_logit = token_logit.reshape(traces, tok_dev)
    partial_logit = jnp.sum(jnp.where(hits, token_logit[:, None, :], 0.0), axis=2)
    logit = over_axes(partial_logit, SEQ_HEAD)
    live = valid == 1
    step_reward = jnp.where(live, logit, jnp.float32(0.0))
    trace_score = jnp.min(jnp.where(live, logit, jnp.float32(1e30)), axis=1)
    trace_ids = jnp.arange(traces, dtype=jnp.int32)[None, :]
    winner = jnp.sum(jnp.where(pairs[:, 0:1] == trace_ids, trace_score[None, :], 0.0), axis=1)
    loser = jnp.sum(jnp.where(pairs[:, 1:2] == trace_ids, trace_score[None, :], 0.0), axis=1)
    return (step_reward, trace_score, winner - loser)


def solution(mesh):
    torus = Mesh(
        mesh.devices.reshape(8, 8, 2, mesh.shape["head"]), ("seq_0", "seq_1", "seq_2", "head")
    )
    return jax.shard_map(
        per_device,
        mesh=torus,
        in_specs=(P(None, SEQ, "head"), P(), P(), P(), P(SEQ, "head"), P("head"), P("head")),
        out_specs=(P(), P(), P()),
        check_vma=False,
    )
```

profile of v0, /device:TPU:1, one launch (start us, length us, event | category | flops | bytes accessed | tf_op | source)
XLA Modules:
  0.0 175.0 jit_solution(17195538024517947789)
XLA Ops:
  7.2 0.0 all-gather.3.cloned.1.call-start
  7.2 0.7 all-gather.3.cloned.1.call-update
  7.9 3.6 %broadcast_in_dim.47 = bf16[4,8,64,896]{3,2,1,0:T(8,128)(2,1)} broadcast(bf16[8,64,896]{2,1,0:T(8,128)(2,1)} %param.7), dimensions={1,2,3} | broadcast | bytes 4587520 | tf_op jit(solution)/shard_map/broadcast_in_dim | solution.py:18
  11.5 0.0 copy-start.3
  11.5 5.0 %all-to-all-start = ((bf16[4,8,64,896]{3,2,1,0:T(8,128)(2,1)}), bf16[4,8,64,896]{3,2,1,0:T(8,128)(2,1)}, u32[]{:S(2)}, u32[]{:S(2)}) async-start(bf16[4,8,64,896]{3,2,1,0:T(8,128)(2,1)} %broadcast_in_dim.47), calls=%async_computation | async-start | bytes 7340032 | tf_op jit(solution)/shard_map/all_to_all | solution.py:19
  16.4 0.0 copy-done.3
  16.4 37.6 %all-to-all-done = bf16[4,8,64,896]{3,2,1,0:T(8,128)(2,1)} async-done(((bf16[4,8,64,896]{3,2,1,0:T(8,128)(2,1)}), bf16[4,8,64,896]{3,2,1,0:T(8,128)(2,1)}, u32[]{:S(2)}, u32[]{:S(2)}) %all-to-all-start) | async-done | bytes 3670048 | tf_op jit(solution)/shard_map/all_to_all | solution.py:19
  54.0 4.9 %copy.11 = bf16[8,64,4,896]{3,2,1,0:T(4,128)(2,1)S(1)} copy(bf16[8,64,4,896]{3,1,0,2:T(8,128)(2,1)} %bitcast) | data formatting | bytes 7340032 | tf_op jit(solution)/shard_map/transpose | solution.py:12
  58.9 2.4 %copy.12 = bf16[64,8,4,896]{3,1,2,0:T(8,128)(2,1)} copy(bf16[64,8,4,896]{3,2,1,0:T(4,128)(2,1)S(1)} %bitcast.11) | data formatting | bytes 7340032
  61.3 0.0 copy-start.4
  61.3 0.0 copy-start.5
  61.3 43.5 %all-gather.3.cloned.1.call-done = bf16[128,28,1024]{2,1,0:T(8,128)(2,1)} async-done(((bf16[1,28,1024]{2,1,0:T(8,128)(2,1)}), bf16[128,28,1024]{2,1,0:T(8,128)(2,1)}) %all-gather.3.cloned.1.call-update) | async-done | bytes 7340048 | tf_op jit(solution)/shard_map/all_gather | solution.py:34
  104.8 10.9 %reshape.16 = bf16[3584,1024]{1,0:T(8,128)(2,1)} reshape(bf16[128,28,1024]{2,1,0:T(8,128)(2,1)} %all-gather.3.cloned.1.call-done) | data formatting | bytes 14680064
  115.7 0.0 copy-done.4
  115.7 0.0 copy-done.5
  115.7 0.0 copy-start
  115.7 0.0 copy-start.1
  115.8 8.3 %multiply_reduce_fusion = f32[512]{0:T(512)S(1)} fusion(bf16[512,3584]{1,0:T(8,128)(2,1)} %bitcast.12, bf16[3584,1024]{1,0:T(8,128)(2,1)} %reshape.16, f32[1024]{0:T(1024)S(1)} %copy-done.4, f32[1024]{0:T(1024)S(1)} %copy-done.5), kind=kOutput, calls=%fused_computation | convolution fusion | flops 3760193024 | bytes 11020288 | tf_op jit(solution)/shard_map/dot_general | solution.py:33
  124.0 0.1 broadcast_in_dim.48
  124.1 0.0 copy-done
  124.1 0.3 select_reduce_fusion
  124.4 12.0 %psum.28 = f32[8,64]{1,0:T(8,128)S(1)} all-reduce(f32[8,64]{1,0:T(8,128)S(1)} %select_reduce_fusion), channel_id=1, replica_groups=mesh['seq_0'=8,'seq_1'=8,'seq_2'=2,'head'=4] {'seq_0'}, use_global_device_ids=true, to_apply=%region_2.3 | all-reduce | flops 512 | bytes 4096 | tf_op jit(solution)/shard_map/psum | solution.py:28
  136.4 12.1 %psum.29 = f32[8,64]{1,0:T(8,128)S(1)} all-reduce(f32[8,64]{1,0:T(8,128)S(1)} %psum.28), channel_id=1, replica_groups=mesh['seq_0'=8,'seq_1'=8,'seq_2'=2,'head'=4] {'seq_1'}, use_global_device_ids=true, to_apply=%region_3.4 | all-reduce | flops 512 | bytes 4096 | tf_op jit(solution)/shard_map/psum | solution.py:28
  148.5 9.8 %psum.30 = f32[8,64]{1,0:T(8,128)S(1)} all-reduce(f32[8,64]{1,0:T(8,128)S(1)} %psum.29), channel_id=1, replica_groups=mesh['seq_0'=8,'seq_1'=8,'seq_2'=2,'head'=4] {'seq_2'}, use_global_device_ids=true, to_apply=%region_4.5 | all-reduce | flops 512 | bytes 4096 | tf_op jit(solution)/shard_map/psum | solution.py:28
  158.3 8.4 %psum.31 = f32[8,64]{1,0:T(8,128)S(1)} all-reduce(f32[8,64]{1,0:T(8,128)S(1)} %psum.30), channel_id=1, replica_groups=mesh['seq_0'=8,'seq_1'=8,'seq_2'=2,'head'=4] {'head'}, use_global_device_ids=true, to_apply=%region_5.6 | all-reduce | flops 512 | bytes 4096 | tf_op jit(solution)/shard_map/psum | solution.py:28
  166.7 0.0 copy-done.1
  166.7 0.1 select_reduce_fusion.3
  166.8 0.0 copy-start.2
  166.8 0.6 broadcast_select_fusion
  167.4 0.2 select_reduce_fusion.1
  167.6 0.5 sub.3
  168.2 0.0 copy-done.2
  (2 shorter events, 0.0 us)
Async XLA Ops:
  7.2 97.6 %all-gather.3.cloned.1.call-start = ((), (), s32[]{:S(2)}) async-start(), calls=%async_computation.1 | async-start | bytes 8454144 | tf_op jit(solution)/shard_map/all_gather | solution.py:34
  11.5 5.0 %copy-start.3 = (s32[8,2]{0,1:T(2,128)S(1)}, s32[8,2]{0,1:T(2,128)}, u32[]{:S(2)}) copy-start(s32[8,2]{0,1:T(2,128)} %param.10) | copy-start | bytes 196
  11.5 42.6 %all-to-all-start = ((bf16[4,8,64,896]{3,2,1,0:T(8,128)(2,1)}), bf16[4,8,64,896]{3,2,1,0:T(8,128)(2,1)}, u32[]{:S(2)}, u32[]{:S(2)}) async-start(bf16[4,8,64,896]{3,2,1,0:T(8,128)(2,1)} %broadcast_in_dim.47), calls=%async_computation | async-start | bytes 7340032 | tf_op jit(solution)/shard_map/all_to_all | solution.py:19
  61.3 54.4 %copy-start.4 = (f32[1024]{0:T(1024)S(1)}, f32[1024]{0:T(1024)}, u32[]{:S(2)}) copy-start(f32[1024]{0:T(1024)} %param.13) | copy-start | bytes 12292
  61.3 54.4 %copy-start.5 = (f32[1024]{0:T(1024)S(1)}, f32[1024]{0:T(1024)}, u32[]{:S(2)}) copy-start(f32[1024]{0:T(1024)} %param.12) | copy-start | bytes 12292
  115.7 8.4 %copy-start = (s32[8,64]{1,0:T(8,128)S(1)}, s32[8,64]{1,0:T(8,128)}, u32[]{:S(2)}) copy-start(s32[8,64]{1,0:T(8,128)} %param.8) | copy-start | bytes 6148
  115.7 51.0 %copy-start.1 = (s32[8,64]{1,0:T(8,128)S(1)}, s32[8,64]{1,0:T(8,128)}, u32[]{:S(2)}) copy-start(s32[8,64]{1,0:T(8,128)} %param.9) | copy-start | bytes 6148
  166.8 1.3 copy-start.2
Sparse Core Ops, SparseCore 0:
  11.1 93.6 all-gather.2
where the time goes:
time: 176 us; the launch traced here: 175 us
  waiting for transfers between devices  81.7 us (46%)
  blocking collectives  42.3 us (24%)
  local copies, waits for them, and re-layouts  21.9 us (12%)
  between operations  14.1 us (8%)
  matrix products  8.25 us (5%)
  starting transfers between devices  5 us (3%)
    all_gather x1, waiting for transfers between devices, score_rows(): lax.all_gather(w_first, SEQ, axis=0, tiled=True)  43.5 us
    psum x4, blocking collectives, over_axes(): shard = lax.psum(shard, axis)  42.3 us
    all_to_all x1, waiting for transfers between devices, sent_to_all(): return lax.all_to_all(copies, axis, split_axis=0, concat_axis=0, tiled=True)  37.6 us
    unnamed x14, local copies, waits for them, and re-layouts  13.4 us
    dot_general x1, matrix products, score_rows(): jnp.dot(rows, lax.all_gather(w_first, SEQ, axis=0, tiled=True), preferred...  8.25 us
    all_to_all x1, starting transfers between devices, sent_to_all(): return lax.all_to_all(copies, axis, split_axis=0, concat_axis=0, tiled=True)  4.96 us
    transpose x1, local copies, waits for them, and re-layouts, laid_out(): pieces = jnp.moveaxis(pieces, 0, dim)  4.88 us
    broadcast_in_dim x1, local copies, waits for them, and re-layouts, sent_to_all(): copies = jnp.broadcast_to(shard, (lax.axis_size(axis), *shard.shape))  3.55 us
  transfers between devices with their start and end apart: 2, of which 2 were waited for; matrix products, arithmetic and copies ran while one was open for 6% of the time, Pallas kernels for 0%

commit v1 on v0

--- a/solution.py
+++ b/solution.py
@@ -31,7 +31,11 @@
 
 def score_rows(rows, w_first, b_first, w_second):
     pre = jnp.dot(
-        rows, lax.all_gather(w_first, SEQ, axis=0, tiled=True), preferred_element_type=jnp.float32
+        rows,
+        jnp.concatenate(
+            lax.all_to_all(jnp.stack([w_first] * lax.axis_size(SEQ)), SEQ, 0, 0), axis=0
+        ),
+        preferred_element_type=jnp.float32,
     )
     return jnp.sum(jnp.maximum(pre + b_first, 0.0) * w_second, axis=-1)
 

time: 176 us -> 403 us (2.29)
  waiting for transfers between devices: 81.7 us -> 218 us
  blocking collectives: 42.3 us -> 125 us
  starting transfers between devices: 5 us -> 23.8 us
  between operations: 14.1 us -> 0.72 us
    all_to_all x1, waiting for transfers between devices: 37.6 us -> 218 us  [score_rows(): lax.all_to_all(jnp.stack([w_first] * lax.axis_size(SEQ)), SEQ, 0, 0)]
    all_gather x1 -> x0, waiting for transfers between devices: 43.5 us -> none  [score_rows(): lax.all_gather(w_first, SEQ, axis=0, tiled=True)]
    all_to_all x0 -> x1, blocking collectives: none -> 42.7 us  [sent_to_all(): return lax.all_to_all(copies, axis, split_axis=0, concat_axis=0, tiled=True)]
    psum x4, blocking collectives: 42.3 us -> 82.1 us  [over_axes(): shard = lax.psum(shard, axis)]
    all_to_all x1, starting transfers between devices: 4.96 us -> 23.8 us  [score_rows(): lax.all_to_all(jnp.stack([w_first] * lax.axis_size(SEQ)), SEQ, 0, 0)]
    unnamed x14 -> x15, local copies, waits for them, and re-layouts: 13.4 us -> 2.42 us
    reshape x0 -> x1, local copies, waits for them, and re-layouts: none -> 10.9 us  [score_rows(): jnp.concatenate(lax.all_to_all(jnp.stack([w_first] * lax.axis_size(SEQ)),...]
    another operation x0 -> x1, local copies, waits for them, and re-layouts: none -> 4.28 us  [score_rows(): jnp.stack([w_first] * lax.axis_size(SEQ))]
  transfers between devices with their start and end apart: 2 -> 1, of which waited for: 2 -> 1; matrix products, arithmetic and copies ran while one was open for 6% -> 2% of each run, Pallas kernels for 0% -> 0%
where the time goes in v1:
time: 403 us; the launch traced here: 402 us
  waiting for transfers between devices  218 us (54%)
  blocking collectives  125 us (31%)
  local copies, waits for them, and re-layouts  24.3 us (6%)
  starting transfers between devices  23.8 us (6%)
  matrix products  8.25 us (2%)
    all_to_all x1, waiting for transfers between devices, score_rows(): lax.all_to_all(jnp.stack([w_first] * lax.axis_size(SEQ)), SEQ, 0, 0)  218 us
    psum x4, blocking collectives, over_axes(): shard = lax.psum(shard, axis)  82.1 us
    all_to_all x1, blocking collectives, sent_to_all(): return lax.all_to_all(copies, axis, split_axis=0, concat_axis=0, tiled=True)  42.7 us
    all_to_all x1, starting transfers between devices, score_rows(): lax.all_to_all(jnp.stack([w_first] * lax.axis_size(SEQ)), SEQ, 0, 0)  23.8 us
    reshape x1, local copies, waits for them, and re-layouts, score_rows(): jnp.concatenate(lax.all_to_all(jnp.stack([w_first] * lax.axis_size(SEQ)),...  10.9 us
    dot_general x1, matrix products, score_rows(): jnp.dot(rows, jnp.concatenate(lax.all_to_all(jnp.stack([w_first] * lax.ax...  8.25 us
  transfers between devices with their start and end apart: 1, of which 1 were waited for; matrix products, arithmetic and copies ran while one was open for 2% of the time, Pallas kernels for 0%

profile of v1, /device:TPU:1, one launch (start us, length us, event | category | flops | bytes accessed | tf_op | source)
XLA Modules:
  0.0 401.7 jit_solution(3544520017725640468)
XLA Ops:
  0.6 1.7 broadcast_in_dim.47
  2.3 0.0 copy-start
  2.3 42.7 %all_to_all.10 = bf16[4,8,64,896]{3,2,1,0:T(8,128)(2,1)} all-to-all(bf16[4,8,64,896]{3,2,1,0:T(8,128)(2,1)S(1)} %broadcast_in_dim.47), channel_id=1, replica_groups=mesh['seq_0'=8,'seq_1'=8,'seq_2'=2,'head'=4] {'head'}, dimensions={0} | all-to-all | bytes 7340032 | tf_op jit(solution)/shard_map/all_to_all | solution.py:19
  45.0 0.0 copy-done
  45.0 4.3 %stack.2 = bf16[128,28,1024]{2,1,0:T(8,128)(2,1)} broadcast(bf16[28,1024]{1,0:T(8,128)(2,1)S(1)} %copy-done), dimensions={1,2} | broadcast | bytes 7397376 | tf_op jit(solution)/shard_map/stack | solution.py:36
  49.3 0.0 copy-start.4
  49.3 23.8 %all-to-all-start.1 = ((bf16[128,28,1024]{2,1,0:T(8,128)(2,1)}), bf16[128,28,1024]{2,1,0:T(8,128)(2,1)}, u32[]{:S(2)}, u32[]{:S(2)}) async-start(bf16[128,28,1024]{2,1,0:T(8,128)(2,1)} %stack.2), calls=%async_computation.1 | async-start | bytes 16777216 | tf_op jit(solution)/shard_map/all_to_all | solution.py:36
  73.2 0.0 copy-done.4
  73.2 4.9 %copy.11 = bf16[8,64,4,896]{3,2,1,0:T(4,128)(2,1)S(1)} copy(bf16[8,64,4,896]{3,1,0,2:T(8,128)(2,1)} %bitcast.10) | data formatting | bytes 7340032 | tf_op jit(solution)/shard_map/transpose | solution.py:12
  78.1 2.4 copy.12
  80.5 0.0 copy-start.5
  80.5 0.0 copy-start.6
  80.5 218.1 %all-to-all-done.1 = bf16[128,28,1024]{2,1,0:T(8,128)(2,1)} async-done(((bf16[128,28,1024]{2,1,0:T(8,128)(2,1)}), bf16[128,28,1024]{2,1,0:T(8,128)(2,1)}, u32[]{:S(2)}, u32[]{:S(2)}) %all-to-all-start.1) | async-done | bytes 7340064 | tf_op jit(solution)/shard_map/all_to_all | solution.py:36
  298.5 10.9 %reshape.20 = bf16[3584,1024]{1,0:T(8,128)(2,1)} reshape(bf16[128,28,1024]{2,1,0:T(8,128)(2,1)} %all-to-all-done.1) | data formatting | bytes 14680064 | tf_op jit(solution)/shard_map/reshape | solution.py:35
  309.5 0.0 copy-done.5
  309.5 0.0 copy-done.6
  309.5 0.0 copy-start.1
  309.5 0.0 copy-start.2
  309.5 8.3 %multiply_reduce_fusion = f32[512]{0:T(512)S(1)} fusion(bf16[512,3584]{1,0:T(8,128)(2,1)} %bitcast.12, bf16[3584,1024]{1,0:T(8,128)(2,1)} %reshape.20, f32[1024]{0:T(1024)S(1)} %copy-done.5, f32[1024]{0:T(1024)S(1)} %copy-done.6), kind=kOutput, calls=%fused_computation | convolution fusion | flops 3760193024 | bytes 11020288 | tf_op jit(solution)/shard_map/dot_general | solution.py:33
  317.8 0.1 broadcast_in_dim.48
  317.8 0.0 copy-done.1
  317.8 0.3 select_reduce_fusion
  318.1 42.8 %psum.28 = f32[8,64]{1,0:T(8,128)S(1)} all-reduce(f32[8,64]{1,0:T(8,128)S(1)} %select_reduce_fusion), channel_id=1, replica_groups=mesh['seq_0'=8,'seq_1'=8,'seq_2'=2,'head'=4] {'seq_0'}, use_global_device_ids=true, to_apply=%region_2.3 | all-reduce | flops 512 | bytes 4096 | tf_op jit(solution)/shard_map/psum | solution.py:28
  360.9 22.4 %psum.29 = f32[8,64]{1,0:T(8,128)S(1)} all-reduce(f32[8,64]{1,0:T(8,128)S(1)} %psum.28), channel_id=1, replica_groups=mesh['seq_0'=8,'seq_1'=8,'seq_2'=2,'head'=4] {'seq_1'}, use_global_device_ids=true, to_apply=%region_3.4 | all-reduce | flops 512 | bytes 4096 | tf_op jit(solution)/shard_map/psum | solution.py:28
  383.3 10.1 %psum.30 = f32[8,64]{1,0:T(8,128)S(1)} all-reduce(f32[8,64]{1,0:T(8,128)S(1)} %psum.29), channel_id=1, replica_groups=mesh['seq_0'=8,'seq_1'=8,'seq_2'=2,'head'=4] {'seq_2'}, use_global_device_ids=true, to_apply=%region_4.5 | all-reduce | flops 512 | bytes 4096 | tf_op jit(solution)/shard_map/psum | solution.py:28
  393.4 6.8 %psum.31 = f32[8,64]{1,0:T(8,128)S(1)} all-reduce(f32[8,64]{1,0:T(8,128)S(1)} %psum.30), channel_id=1, replica_groups=mesh['seq_0'=8,'seq_1'=8,'seq_2'=2,'head'=4] {'head'}, use_global_device_ids=true, to_apply=%region_5.6 | all-reduce | flops 512 | bytes 4096 | tf_op jit(solution)/shard_map/psum | solution.py:28
  400.3 0.0 copy-done.2
  400.3 0.1 select_reduce_fusion.3
  400.4 0.0 copy-start.3
  400.4 0.6 broadcast_select_fusion
  401.0 0.2 select_reduce_fusion.1
  401.2 0.5 sub.3
  401.7 0.0 copy-done.3
  (2 shorter events, 0.0 us)
Async XLA Ops:
  2.3 42.7 %copy-start = (bf16[28,1024]{1,0:T(8,128)(2,1)S(1)}, bf16[28,1024]{1,0:T(8,128)(2,1)}, u32[]{:S(2)}) copy-start(bf16[28,1024]{1,0:T(8,128)(2,1)} %param.11) | copy-start | bytes 172036
  49.3 23.9 %copy-start.4 = (s32[8,2]{0,1:T(2,128)S(1)}, s32[8,2]{0,1:T(2,128)}, u32[]{:S(2)}) copy-start(s32[8,2]{0,1:T(2,128)} %param.10) | copy-start | bytes 196
  49.3 249.2 %all-to-all-start.1 = ((bf16[128,28,1024]{2,1,0:T(8,128)(2,1)}), bf16[128,28,1024]{2,1,0:T(8,128)(2,1)}, u32[]{:S(2)}, u32[]{:S(2)}) async-start(bf16[128,28,1024]{2,1,0:T(8,128)(2,1)} %stack.2), calls=%async_computation.1 | async-start | bytes 16777216 | tf_op jit(solution)/shard_map/all_to_all | solution.py:36
  80.5 229.0 %copy-start.5 = (f32[1024]{0:T(1024)S(1)}, f32[1024]{0:T(1024)}, u32[]{:S(2)}) copy-start(f32[1024]{0:T(1024)} %param.13) | copy-start | bytes 12292
  80.5 229.0 %copy-start.6 = (f32[1024]{0:T(1024)S(1)}, f32[1024]{0:T(1024)}, u32[]{:S(2)}) copy-start(f32[1024]{0:T(1024)} %param.12) | copy-start | bytes 12292
  309.5 8.4 %copy-start.1 = (s32[8,64]{1,0:T(8,128)S(1)}, s32[8,64]{1,0:T(8,128)}, u32[]{:S(2)}) copy-start(s32[8,64]{1,0:T(8,128)} %param.8) | copy-start | bytes 6148
  309.5 90.8 %copy-start.2 = (s32[8,64]{1,0:T(8,128)S(1)}, s32[8,64]{1,0:T(8,128)}, u32[]{:S(2)}) copy-start(s32[8,64]{1,0:T(8,128)} %param.9) | copy-start | bytes 6148
  400.4 1.3 copy-start.3
